TPU v7x, 32 devices: a whole 2x2x4 slice. The times are simulated.
32 devices in a mesh: grp: 2 (over y), gx: 4 (over z), gy: 2 (over x), gz: 2 (over core).
Axes of the slice: x: 2, y: 2, z: 4, core: 2. Of those that a mesh axis runs over, the one named last changes fastest.
Arguments:
- position: float32 [64, 16, 4, 256], P(None, ('grp', 'gx'), 'gy', 'gz'), parts along dimension 1, may hold values from -6 to 6
- momentum: float32 [64, 16, 4, 256], P(None, ('grp', 'gx'), 'gy', 'gz'), parts along dimension 1, may hold values from -6 to 6
- noise: bfloat16 [3, 64, 16, 4, 256], P(None, None, ('grp', 'gx'), 'gy', 'gz'), parts along dimension 2, may hold values from -6 to 6
- filter_in: bfloat16 [64, 64, 3, 3, 3], P('gx', 'gy'), may hold values from -0.15625 to 0.15625
- filter_out: bfloat16 [64, 64, 3, 3, 3], P('gx', 'gy'), may hold values from -0.15625 to 0.15625
- bias: float32 [64], replicated, may hold values from -4 to 4
Outputs:
- final_position: float32 [64, 16, 4, 256], P(None, ('grp', 'gx'), 'gy', 'gz'), parts along dimension 1
- final_momentum: float32 [64, 16, 4, 256], P(None, ('grp', 'gx'), 'gy', 'gz'), parts along dimension 1
There are 2 independent parts, one for each index of `grp`. A program takes and returns all parts, laid end to end along the dimension named above; an argument that names none is the same for every part. Nothing has to cross between parts.
All inputs are finite; a program needn't handle non-finite values.
Results may differ from a plain program's by a relative error of at most 0.0013.
Values may be sent and summed in bfloat16 or wider, within the bound.
A program may use at most 64 MiB of HBM per device.

v0:
```python
import jax
import jax.numpy as jnp
from jax import lax
from jax.sharding import PartitionSpec as P


def padded_2(block, sides, width):
    for axis, dim in sides:
        count = lax.axis_size(axis)
        forward = [(i, i + 1) for i in range(count - 1)]
        forward.append((count - 1, 0))
        backward = [(target, source) for source, target in forward]
        low = lax.ppermute(
            lax.slice_in_dim(block, block.shape[dim] - width, None, axis=dim), axis, forward
        )
        high = lax.ppermute(lax.slice_in_dim(block, 0, width, axis=dim), axis, backward)
        block = jnp.concatenate([low, block, high], axis=dim)
    return block


def convolve(padded, filters):
    return lax.conv_general_dilated(
        padded[None],
        filters,
        (1, 1, 1),
        "VALID",
        dimension_numbers=("NCDHW", "OIDHW", "NCDHW"),
        preferred_element_type=jnp.float32,
    )[0]


def adjoint(filters):
    return jnp.transpose(jnp.flip(filters, (2, 3, 4)), (1, 0, 2, 3, 4))


def on_device(position, momentum, noise, filter_in, filter_out, bias):
    rows = (
        lax.all_gather(filter_in, "gx", axis=0, tiled=True),
        lax.all_gather(filter_out, "gx", axis=0, tiled=True),
    )
    first, second = (
        lax.all_gather(rows[0], "gy", axis=1, tiled=True),
        lax.all_gather(rows[1], "gy", axis=1, tiled=True),
    )
    back_in = adjoint(first)
    back_out = adjoint(second)
    bias_col = bias[:, None, None, None]

    def gradient(field):
        rounded = field.astype(jnp.bfloat16)
        band = padded_2(rounded, (("gx", 1), ("gy", 2), ("gz", 3)), 2)
        active = jnp.tanh(convolve(band, first) + bias_col)
        output = convolve(active.astype(jnp.bfloat16), second).astype(jnp.bfloat16)
        outer = padded_2(output, (("gx", 1), ("gy", 2), ("gz", 3)), 2)
        back = convolve(outer, back_out)
        hidden = (back * (1.0 - active * active)).astype(jnp.bfloat16)
        return convolve(hidden, back_in) + field

    step = 0.25
    decay = jnp.exp(jnp.float32(-0.25))
    kick = jnp.sqrt(1.0 - decay * decay)
    field = position
    moment = momentum
    force = gradient(field)
    for index in range(noise.shape[0]):
        moment = moment - 0.5 * step * force
        field = field + 0.5 * step * moment
        moment = decay * moment + kick * noise[index].astype(jnp.float32)
        field = field + 0.5 * step * moment
        force = gradient(field)
        moment = moment - 0.5 * step * force
    return (field, moment)


def solution(mesh):
    in_specs = (
        P(None, ("grp", "gx"), "gy", "gz"),
        P(None, ("grp", "gx"), "gy", "gz"),
        P(None, None, ("grp", "gx"), "gy", "gz"),
        P("gx", "gy", None, None, None),
        P("gx", "gy", None, None, None),
        P(),
    )
    out_specs = (P(None, ("grp", "gx"), "gy", "gz"), P(None, ("grp", "gx"), "gy", "gz"))
    return jax.shard_map(
        on_device, mesh=mesh, in_specs=in_specs, out_specs=out_specs, check_vma=False
    )
```

profile of v0, /device:TPU:0, one launch (start us, length us, event | category | flops | bytes accessed | tf_op | source)
XLA Modules:
  0.0 313.7 jit_solution(4875933987798309094)
XLA Ops:
  1.7 3.1 collective-permute-start
  6.9 4.3 %collective-permute-done = bf16[64,2,2,128]{0,2,3,1:T(2,128)(2,1)S(1)} collective-permute-done((bf16[64,2,2,128]{0,2,3,1:T(2,128)(2,1)S(1)}, bf16[64,2,2,128]{0,2,3,1:T(2,128)(2,1)S(1)}, u32[]{:S(2)}, u32[]{:S(2)}) %collective-permute-start) | collective-permute-done | bytes 65568 | tf_op jit(solution)/shard_map/ppermute | solution.py:13
  15.4 15.5 %all_gather.12 = bf16[64,32,3,3,3]{1,0,4,3,2:T(8,128)(2,1)S(1)} all-gather(bf16[16,32,3,3,3]{1,0,4,3,2:T(8,128)(2,1)} %param.9), channel_id=1, replica_groups=mesh['grp'=2,'gx'=4,'gy'=2,'gz'=2] {'gx'}, dimensions={0}, use_global_device_ids=true | all-gather | bytes 138240 | tf_op jit(solution)/shard_map/all_gather | solution.py:38
  31.0 14.5 %all_gather.14 = bf16[64,32,3,3,3]{1,0,4,3,2:T(8,128)(2,1)S(1)} all-gather(bf16[16,32,3,3,3]{1,0,4,3,2:T(8,128)(2,1)S(1)} %copy-done.20), channel_id=1, replica_groups=mesh['grp'=2,'gx'=4,'gy'=2,'gz'=2] {'gx'}, dimensions={0}, use_global_device_ids=true | all-gather | bytes 138240 | tf_op jit(solution)/shard_map/all_gather | solution.py:39
  45.7 6.6 %all_gather.13 = bf16[64,64,3,3,3]{0,1,4,3,2:T(8,128)(2,1)S(1)} all-gather(bf16[64,32,3,3,3]{0,1,4,3,2:T(8,128)(2,1)S(1)} %copy.283), channel_id=1, replica_groups=mesh['grp'=2,'gx'=4,'gy'=2,'gz'=2] {'gy'}, dimensions={1}, use_global_device_ids=true | all-gather | bytes 331776 | tf_op jit(solution)/shard_map/all_gather | solution.py:42
  53.0 8.1 %all_gather.15 = bf16[64,64,3,3,3]{0,1,4,3,2:T(8,128)(2,1)S(1)} all-gather(bf16[64,32,3,3,3]{0,1,4,3,2:T(8,128)(2,1)S(1)} %copy.284), channel_id=1, replica_groups=mesh['grp'=2,'gx'=4,'gy'=2,'gz'=2] {'gy'}, dimensions={1}, use_global_device_ids=true | all-gather | bytes 331776 | tf_op jit(solution)/shard_map/all_gather | solution.py:43
  72.2 4.0 %collective-permute-done.6 = bf16[64,2,2,128]{0,2,3,1:T(2,128)(2,1)S(1)} collective-permute-done((bf16[64,2,2,128]{0,2,3,1:T(2,128)(2,1)S(1)}, bf16[64,2,2,128]{0,2,3,1:T(2,128)(2,1)S(1)}, u32[]{:S(2)}, u32[]{:S(2)}) %collective-permute-start.6) | collective-permute-done | bytes 65568 | tf_op jit(solution)/shard_map/ppermute | solution.py:13
  79.8 10.0 %collective-permute-done.8 = bf16[64,6,2,128]{0,2,3,1:T(2,128)(2,1)S(1)} collective-permute-done((bf16[64,6,2,128]{0,2,3,1:T(2,128)(2,1)S(1)}, bf16[64,6,2,128]{0,2,3,1:T(2,128)(2,1)S(1)}, u32[]{:S(2)}, u32[]{:S(2)}) %collective-permute-start.8) | collective-permute-done | bytes 196640 | tf_op jit(solution)/shard_map/ppermute | solution.py:13
  89.8 6.9 %collective-permute-done.9 = bf16[64,6,2,128]{0,2,3,1:T(2,128)(2,1)S(1)} collective-permute-done((bf16[64,6,2,128]{0,2,3,1:T(2,128)(2,1)S(1)}, bf16[64,6,2,128]{0,2,3,1:T(2,128)(2,1)S(1)}, u32[]{:S(2)}, u32[]{:S(2)}) %collective-permute-start.9) | collective-permute-done | bytes 196640 | tf_op jit(solution)/shard_map/ppermute | solution.py:16
  101.4 4.1 %fusion.156 = bf16[4,4,1,8,17,64]{5,3,4,1,0,2:T(8,128)(2,1)S(1)} fusion(bf16[64,64,3,3,3]{0,1,4,3,2:T(8,128)(2,1)S(1)} %all_gather.15, bf16[64,6,6,1,7,2]{0,4,5,2,1,3:T(8,128)(2,1)S(1)} %slice.103, bf16[64,6,6,1,8,17]{0,4,5,2,1,3:T(8,128)(2,1)S(1)} %copy.292, f32[4,4,8,17,64]{4,2,3,1,0:T(8,128)S(1)} %fusion.103, pred[8,17]{0,1:T(8,128)(4,1)S(1)} %copy-done.21), kind=kOutput, calls=%fused_computation.99 | convolution fusion | flops 484233216 | bytes 1748104 | tf_op jit(solution)/shard_map/conv_general_dilated | solution.py:22
  108.7 3.1 collective-permute-start.13
  116.8 5.7 %collective-permute-done.14 = bf16[64,6,2,128]{3,0,2,1:T(8,128)(2,1)S(1)} collective-permute-done((bf16[64,6,2,128]{3,0,2,1:T(8,128)(2,1)S(1)}, bf16[64,6,2,128]{3,0,2,1:T(8,128)(2,1)S(1)}, u32[]{:S(2)}, u32[]{:S(2)}) %collective-permute-start.14) | collective-permute-done | bytes 196640 | tf_op jit(solution)/shard_map/ppermute | solution.py:13
  135.0 4.3 %collective-permute-start.19 = (bf16[64,2,2,128]{0,2,3,1:T(2,128)(2,1)S(1)}, bf16[64,2,2,128]{0,2,3,1:T(2,128)(2,1)S(1)}, u32[]{:S(2)}, u32[]{:S(2)}) collective-permute-start(bf16[64,2,2,128]{0,2,3,1:T(2,128)(2,1)S(1)} %slice_bitcast_fusion.2), channel_id=1, source_target_pairs={{4,0},{8,4},{12,8},{0,12},{5,1},{9,5},{13,9},{1,13},{6,2},{10,6},{... | collective-permute-start | bytes 196616 | tf_op jit(solution)/shard_map/ppermute | solution.py:16
  139.2 3.9 %collective-permute-done.18 = bf16[64,2,2,128]{0,2,3,1:T(2,128)(2,1)S(1)} collective-permute-done((bf16[64,2,2,128]{0,2,3,1:T(2,128)(2,1)S(1)}, bf16[64,2,2,128]{0,2,3,1:T(2,128)(2,1)S(1)}, u32[]{:S(2)}, u32[]{:S(2)}) %collective-permute-start.18) | collective-permute-done | bytes 65568 | tf_op jit(solution)/shard_map/ppermute | solution.py:13
  147.2 10.0 %collective-permute-done.20 = bf16[64,6,2,128]{0,2,3,1:T(2,128)(2,1)S(1)} collective-permute-done((bf16[64,6,2,128]{0,2,3,1:T(2,128)(2,1)S(1)}, bf16[64,6,2,128]{0,2,3,1:T(2,128)(2,1)S(1)}, u32[]{:S(2)}, u32[]{:S(2)}) %collective-permute-start.20) | collective-permute-done | bytes 196640 | tf_op jit(solution)/shard_map/ppermute | solution.py:13
  157.2 6.9 %collective-permute-done.21 = bf16[64,6,2,128]{0,2,3,1:T(2,128)(2,1)S(1)} collective-permute-done((bf16[64,6,2,128]{0,2,3,1:T(2,128)(2,1)S(1)}, bf16[64,6,2,128]{0,2,3,1:T(2,128)(2,1)S(1)}, u32[]{:S(2)}, u32[]{:S(2)}) %collective-permute-start.21) | collective-permute-done | bytes 196640 | tf_op jit(solution)/shard_map/ppermute | solution.py:16
  168.8 4.1 %fusion.159 = bf16[4,4,1,8,17,64]{5,3,4,1,0,2:T(8,128)(2,1)S(1)} fusion(bf16[64,64,3,3,3]{0,1,4,3,2:T(8,128)(2,1)S(1)} %copy-done.16, bf16[64,6,6,1,7,2]{0,4,5,2,1,3:T(8,128)(2,1)S(1)} %slice.111, bf16[64,6,6,1,8,17]{0,4,5,2,1,3:T(8,128)(2,1)S(1)} %copy.313, f32[4,4,8,17,64]{4,2,3,1,0:T(8,128)S(1)} %fusion.109, pred[8,17]{0,1:T(8,128)(4,1)S(1)} %copy-done.21), kind=kOutput, calls=%fused_computation.100 | convolution fusion | flops 484233216 | bytes 1748104 | tf_op jit(solution)/shard_map/conv_general_dilated | solution.py:22
  179.2 2.8 collective-permute-done.24
  184.9 5.7 %collective-permute-done.26 = bf16[64,6,2,128]{3,0,2,1:T(8,128)(2,1)S(1)} collective-permute-done((bf16[64,6,2,128]{3,0,2,1:T(8,128)(2,1)S(1)}, bf16[64,6,2,128]{3,0,2,1:T(8,128)(2,1)S(1)}, u32[]{:S(2)}, u32[]{:S(2)}) %collective-permute-start.26) | collective-permute-done | bytes 196640 | tf_op jit(solution)/shard_map/ppermute | solution.py:13
  190.7 3.2 %collective-permute-done.27 = bf16[64,6,2,128]{3,0,2,1:T(8,128)(2,1)S(1)} collective-permute-done((bf16[64,6,2,128]{3,0,2,1:T(8,128)(2,1)S(1)}, bf16[64,6,2,128]{3,0,2,1:T(8,128)(2,1)S(1)}, u32[]{:S(2)}, u32[]{:S(2)}) %collective-permute-start.27) | collective-permute-done | bytes 196640 | tf_op jit(solution)/shard_map/ppermute | solution.py:16
  204.6 3.7 %collective-permute-start.31 = (bf16[64,2,2,128]{0,2,3,1:T(2,128)(2,1)S(1)}, bf16[64,2,2,128]{0,2,3,1:T(2,128)(2,1)S(1)}, u32[]{:S(2)}, u32[]{:S(2)}) collective-permute-start(bf16[64,2,2,128]{0,2,3,1:T(2,128)(2,1)S(1)} %slice_bitcast_fusion.1), channel_id=1, source_target_pairs={{4,0},{8,4},{12,8},{0,12},{5,1},{9,5},{13,9},{1,13},{6,2},{10,6},{... | collective-permute-start | bytes 196616 | tf_op jit(solution)/shard_map/ppermute | solution.py:16
  208.3 4.2 %collective-permute-done.30 = bf16[64,2,2,128]{0,2,3,1:T(2,128)(2,1)S(1)} collective-permute-done((bf16[64,2,2,128]{0,2,3,1:T(2,128)(2,1)S(1)}, bf16[64,2,2,128]{0,2,3,1:T(2,128)(2,1)S(1)}, u32[]{:S(2)}, u32[]{:S(2)}) %collective-permute-start.30) | collective-permute-done | bytes 65568 | tf_op jit(solution)/shard_map/ppermute | solution.py:13
  215.9 10.0 %collective-permute-done.32 = bf16[64,6,2,128]{0,2,3,1:T(2,128)(2,1)S(1)} collective-permute-done((bf16[64,6,2,128]{0,2,3,1:T(2,128)(2,1)S(1)}, bf16[64,6,2,128]{0,2,3,1:T(2,128)(2,1)S(1)}, u32[]{:S(2)}, u32[]{:S(2)}) %collective-permute-start.32) | collective-permute-done | bytes 196640 | tf_op jit(solution)/shard_map/ppermute | solution.py:13
  225.8 6.5 %collective-permute-done.33 = bf16[64,6,2,128]{0,2,3,1:T(2,128)(2,1)S(1)} collective-permute-done((bf16[64,6,2,128]{0,2,3,1:T(2,128)(2,1)S(1)}, bf16[64,6,2,128]{0,2,3,1:T(2,128)(2,1)S(1)}, u32[]{:S(2)}, u32[]{:S(2)}) %collective-permute-start.33) | collective-permute-done | bytes 196640 | tf_op jit(solution)/shard_map/ppermute | solution.py:16
  237.0 4.1 %fusion.162 = bf16[4,4,1,8,17,64]{5,3,4,1,0,2:T(8,128)(2,1)S(1)} fusion(bf16[64,64,3,3,3]{0,1,4,3,2:T(8,128)(2,1)S(1)} %copy-done.17, bf16[64,6,6,1,7,2]{0,4,5,2,1,3:T(8,128)(2,1)S(1)} %slice.119, bf16[64,6,6,1,8,17]{0,4,5,2,1,3:T(8,128)(2,1)S(1)} %copy.331, f32[4,4,8,17,64]{4,2,3,1,0:T(8,128)S(1)} %fusion.115, pred[8,17]{0,1:T(8,128)(4,1)S(1)} %copy-done.21), kind=kOutput, calls=%fused_computation.101 | convolution fusion | flops 484233216 | bytes 1748104 | tf_op jit(solution)/shard_map/conv_general_dilated | solution.py:22
  244.5 3.5 %collective-permute-start.37 = (bf16[64,2,2,128]{3,0,2,1:T(8,128)(2,1)S(1)}, bf16[64,2,2,128]{3,0,2,1:T(8,128)(2,1)S(1)}, u32[]{:S(2)}, u32[]{:S(2)}) collective-permute-start(bf16[64,2,2,128]{3,0,2,1:T(8,128)(2,1)S(1)} %get-tuple-element.12), channel_id=1, source_target_pairs={{4,0},{8,4},{12,8},{0,12},{5,1},{9,5},{13,9},{1,13},{6,2},{10,6},{... | collective-permute-start | bytes 196616 | tf_op jit(solution)/shard_map/ppermute | solution.py:16
  253.1 5.7 %collective-permute-done.38 = bf16[64,6,2,128]{3,0,2,1:T(8,128)(2,1)S(1)} collective-permute-done((bf16[64,6,2,128]{3,0,2,1:T(8,128)(2,1)S(1)}, bf16[64,6,2,128]{3,0,2,1:T(8,128)(2,1)S(1)}, u32[]{:S(2)}, u32[]{:S(2)}) %collective-permute-start.38) | collective-permute-done | bytes 196640 | tf_op jit(solution)/shard_map/ppermute | solution.py:13
  273.2 2.7 collective-permute-start.43
  275.9 4.1 %collective-permute-done.42 = bf16[64,2,2,128]{0,2,3,1:T(2,128)(2,1)S(1)} collective-permute-done((bf16[64,2,2,128]{0,2,3,1:T(2,128)(2,1)S(1)}, bf16[64,2,2,128]{0,2,3,1:T(2,128)(2,1)S(1)}, u32[]{:S(2)}, u32[]{:S(2)}) %collective-permute-start.42) | collective-permute-done | bytes 65568 | tf_op jit(solution)/shard_map/ppermute | solution.py:13
  284.5 10.0 %collective-permute-done.44 = bf16[64,6,2,128]{0,2,3,1:T(2,128)(2,1)S(1)} collective-permute-done((bf16[64,6,2,128]{0,2,3,1:T(2,128)(2,1)S(1)}, bf16[64,6,2,128]{0,2,3,1:T(2,128)(2,1)S(1)}, u32[]{:S(2)}, u32[]{:S(2)}) %collective-permute-start.44) | collective-permute-done | bytes 196640 | tf_op jit(solution)/shard_map/ppermute | solution.py:13
  294.5 7.0 %collective-permute-done.45 = bf16[64,6,2,128]{0,2,3,1:T(2,128)(2,1)S(1)} collective-permute-done((bf16[64,6,2,128]{0,2,3,1:T(2,128)(2,1)S(1)}, bf16[64,6,2,128]{0,2,3,1:T(2,128)(2,1)S(1)}, u32[]{:S(2)}, u32[]{:S(2)}) %collective-permute-start.45) | collective-permute-done | bytes 196640 | tf_op jit(solution)/shard_map/ppermute | solution.py:16
  306.2 4.1 %fusion.165 = bf16[4,4,1,8,17,64]{5,3,4,1,0,2:T(8,128)(2,1)S(1)} fusion(bf16[64,64,3,3,3]{0,1,4,3,2:T(8,128)(2,1)S(1)} %copy-done.18, bf16[64,6,6,1,7,2]{0,4,5,2,1,3:T(8,128)(2,1)S(1)} %slice.127, bf16[64,6,6,1,8,17]{0,4,5,2,1,3:T(8,128)(2,1)S(1)} %copy.349, f32[4,4,8,17,64]{4,2,3,1,0:T(8,128)S(1)} %fusion.121, pred[8,17]{0,1:T(8,128)(4,1)S(1)} %copy-done.21), kind=kOutput, calls=%fused_computation.102 | convolution fusion | flops 484233216 | bytes 1748104 | tf_op jit(solution)/shard_map/conv_general_dilated | solution.py:22
  (257 shorter events, 119.1 us)
Async XLA Ops:
  1.7 9.5 %collective-permute-start = (bf16[64,2,2,128]{0,2,3,1:T(2,128)(2,1)S(1)}, bf16[64,2,2,128]{0,2,3,1:T(2,128)(2,1)S(1)}, u32[]{:S(2)}, u32[]{:S(2)}) collective-permute-start(bf16[64,2,2,128]{0,2,3,1:T(2,128)(2,1)S(1)} %copy.279), channel_id=1, source_target_pairs={{0,4},{4,8},{8,12},{12,0},{1,5},{5,9},{9,13},{13,1},{2,6},{6,10},{... | collective-permute-start | bytes 196616 | tf_op jit(solution)/shard_map/ppermute | solution.py:13
  4.8 7.8 %collective-permute-start.1 = (bf16[64,2,2,128]{0,2,3,1:T(2,128)(2,1)S(1)}, bf16[64,2,2,128]{0,2,3,1:T(2,128)(2,1)S(1)}, u32[]{:S(2)}, u32[]{:S(2)}) collective-permute-start(bf16[64,2,2,128]{0,2,3,1:T(2,128)(2,1)S(1)} %copy.279), channel_id=1, source_target_pairs={{4,0},{8,4},{12,8},{0,12},{5,1},{9,5},{13,9},{1,13},{6,2},{10,6},{... | collective-permute-start | bytes 196616 | tf_op jit(solution)/shard_map/ppermute | solution.py:16
  13.3 39.1 %collective-permute-start.2 = (bf16[64,6,2,128]{0,2,3,1:T(2,128)(2,1)S(1)}, bf16[64,6,2,128]{0,2,3,1:T(2,128)(2,1)S(1)}, u32[]{:S(2)}, u32[]{:S(2)}) collective-permute-start(bf16[64,6,2,128]{0,2,3,1:T(2,128)(2,1)S(1)} %pad_maximum_fusion.3), channel_id=1, source_target_pairs={{0,2},{2,0},{1,3},{3,1},{4,6},{6,4},{5,7},{7,5},{8,10},{10,8},{9,1... | collective-permute-start | bytes 589832 | tf_op jit(solution)/shard_map/ppermute | solution.py:13
  14.8 37.5 %collective-permute-start.3 = (bf16[64,6,2,128]{0,2,3,1:T(2,128)(2,1)S(1)}, bf16[64,6,2,128]{0,2,3,1:T(2,128)(2,1)S(1)}, u32[]{:S(2)}, u32[]{:S(2)}) collective-permute-start(bf16[64,6,2,128]{0,2,3,1:T(2,128)(2,1)S(1)} %pad_maximum_fusion.3), channel_id=1, source_target_pairs={{2,0},{0,2},{3,1},{1,3},{6,4},{4,6},{7,5},{5,7},{10,8},{8,10},{11,... | collective-permute-start | bytes 589832 | tf_op jit(solution)/shard_map/ppermute | solution.py:16
  52.4 8.6 %collective-permute-start.4 = (bf16[64,6,6,2]{0,2,3,1:T(8,128)(2,1)S(1)}, bf16[64,6,6,2]{0,2,3,1:T(8,128)(2,1)S(1)}, u32[]{:S(2)}, u32[]{:S(2)}) collective-permute-start(bf16[64,6,6,2]{0,2,3,1:T(8,128)(2,1)S(1)} %get-tuple-element.26), channel_id=1, source_target_pairs={{0,1},{1,0},{2,3},{3,2},{4,5},{5,4},{6,7},{7,6},{8,9},{9,8},{10,11... | collective-permute-start | bytes 27656 | tf_op jit(solution)/shard_map/ppermute | solution.py:13
  52.5 8.6 %collective-permute-start.5 = (bf16[64,6,6,2]{0,2,3,1:T(8,128)(2,1)S(1)}, bf16[64,6,6,2]{0,2,3,1:T(8,128)(2,1)S(1)}, u32[]{:S(2)}, u32[]{:S(2)}) collective-permute-start(bf16[64,6,6,2]{0,2,3,1:T(8,128)(2,1)S(1)} %get-tuple-element.27), channel_id=1, source_target_pairs={{1,0},{0,1},{3,2},{2,3},{5,4},{4,5},{7,6},{6,7},{9,8},{8,9},{11,10... | collective-permute-start | bytes 27656 | tf_op jit(solution)/shard_map/ppermute | solution.py:16
  68.1 8.1 %collective-permute-start.6 = (bf16[64,2,2,128]{0,2,3,1:T(2,128)(2,1)S(1)}, bf16[64,2,2,128]{0,2,3,1:T(2,128)(2,1)S(1)}, u32[]{:S(2)}, u32[]{:S(2)}) collective-permute-start(bf16[64,2,2,128]{0,2,3,1:T(2,128)(2,1)S(1)} %slice_bitcast_fusion.3), channel_id=1, source_target_pairs={{0,4},{4,8},{8,12},{12,0},{1,5},{5,9},{9,13},{13,1},{2,6},{6,10},{... | collective-permute-start | bytes 196616 | tf_op jit(solution)/shard_map/ppermute | solution.py:13
  69.7 7.3 %collective-permute-start.7 = (bf16[64,2,2,128]{0,2,3,1:T(2,128)(2,1)S(1)}, bf16[64,2,2,128]{0,2,3,1:T(2,128)(2,1)S(1)}, u32[]{:S(2)}, u32[]{:S(2)}) collective-permute-start(bf16[64,2,2,128]{0,2,3,1:T(2,128)(2,1)S(1)} %slice_bitcast_fusion.3), channel_id=1, source_target_pairs={{4,0},{8,4},{12,8},{0,12},{5,1},{9,5},{13,9},{1,13},{6,2},{10,6},{... | collective-permute-start | bytes 196616 | tf_op jit(solution)/shard_map/ppermute | solution.py:16
  77.7 12.1 %collective-permute-start.8 = (bf16[64,6,2,128]{0,2,3,1:T(2,128)(2,1)S(1)}, bf16[64,6,2,128]{0,2,3,1:T(2,128)(2,1)S(1)}, u32[]{:S(2)}, u32[]{:S(2)}) collective-permute-start(bf16[64,6,2,128]{0,2,3,1:T(2,128)(2,1)S(1)} %pad_maximum_fusion.4), channel_id=1, source_target_pairs={{0,2},{2,0},{1,3},{3,1},{4,6},{6,4},{5,7},{7,5},{8,10},{10,8},{9,1... | collective-permute-start | bytes 589832 | tf_op jit(solution)/shard_map/ppermute | solution.py:13
  79.3 17.4 %collective-permute-start.9 = (bf16[64,6,2,128]{0,2,3,1:T(2,128)(2,1)S(1)}, bf16[64,6,2,128]{0,2,3,1:T(2,128)(2,1)S(1)}, u32[]{:S(2)}, u32[]{:S(2)}) collective-permute-start(bf16[64,6,2,128]{0,2,3,1:T(2,128)(2,1)S(1)} %pad_maximum_fusion.4), channel_id=1, source_target_pairs={{2,0},{0,2},{3,1},{1,3},{6,4},{4,6},{7,5},{5,7},{10,8},{8,10},{11,... | collective-permute-start | bytes 589832 | tf_op jit(solution)/shard_map/ppermute | solution.py:16
  107.7 6.8 %collective-permute-start.12 = (bf16[64,2,2,128]{3,0,2,1:T(8,128)(2,1)S(1)}, bf16[64,2,2,128]{3,0,2,1:T(8,128)(2,1)S(1)}, u32[]{:S(2)}, u32[]{:S(2)}) collective-permute-start(bf16[64,2,2,128]{3,0,2,1:T(8,128)(2,1)S(1)} %get-tuple-element.16), channel_id=1, source_target_pairs={{0,4},{4,8},{8,12},{12,0},{1,5},{5,9},{9,13},{13,1},{2,6},{6,10},{... | collective-permute-start | bytes 196616 | tf_op jit(solution)/shard_map/ppermute | solution.py:13
  114.7 7.8 %collective-permute-start.14 = (bf16[64,6,2,128]{3,0,2,1:T(8,128)(2,1)S(1)}, bf16[64,6,2,128]{3,0,2,1:T(8,128)(2,1)S(1)}, u32[]{:S(2)}, u32[]{:S(2)}) collective-permute-start(bf16[64,6,2,128]{3,0,2,1:T(8,128)(2,1)S(1)} %pad_maximum_fusion.8), channel_id=1, source_target_pairs={{0,2},{2,0},{1,3},{3,1},{4,6},{6,4},{5,7},{7,5},{8,10},{10,8},{9,1... | collective-permute-start | bytes 589832 | tf_op jit(solution)/shard_map/ppermute | solution.py:13
  116.2 8.3 %collective-permute-start.15 = (bf16[64,6,2,128]{3,0,2,1:T(8,128)(2,1)S(1)}, bf16[64,6,2,128]{3,0,2,1:T(8,128)(2,1)S(1)}, u32[]{:S(2)}, u32[]{:S(2)}) collective-permute-start(bf16[64,6,2,128]{3,0,2,1:T(8,128)(2,1)S(1)} %pad_maximum_fusion.8), channel_id=1, source_target_pairs={{2,0},{0,2},{3,1},{1,3},{6,4},{4,6},{7,5},{5,7},{10,8},{8,10},{11,... | collective-permute-start | bytes 589832 | tf_op jit(solution)/shard_map/ppermute | solution.py:16
  134.9 8.2 %collective-permute-start.18 = (bf16[64,2,2,128]{0,2,3,1:T(2,128)(2,1)S(1)}, bf16[64,2,2,128]{0,2,3,1:T(2,128)(2,1)S(1)}, u32[]{:S(2)}, u32[]{:S(2)}) collective-permute-start(bf16[64,2,2,128]{0,2,3,1:T(2,128)(2,1)S(1)} %slice_bitcast_fusion.2), channel_id=1, source_target_pairs={{0,4},{4,8},{8,12},{12,0},{1,5},{5,9},{9,13},{13,1},{2,6},{6,10},{... | collective-permute-start | bytes 196616 | tf_op jit(solution)/shard_map/ppermute | solution.py:13
  135.0 9.5 %collective-permute-start.19 = (bf16[64,2,2,128]{0,2,3,1:T(2,128)(2,1)S(1)}, bf16[64,2,2,128]{0,2,3,1:T(2,128)(2,1)S(1)}, u32[]{:S(2)}, u32[]{:S(2)}) collective-permute-start(bf16[64,2,2,128]{0,2,3,1:T(2,128)(2,1)S(1)} %slice_bitcast_fusion.2), channel_id=1, source_target_pairs={{4,0},{8,4},{12,8},{0,12},{5,1},{9,5},{13,9},{1,13},{6,2},{10,6},{... | collective-permute-start | bytes 196616 | tf_op jit(solution)/shard_map/ppermute | solution.py:16
  145.1 12.1 %collective-permute-start.20 = (bf16[64,6,2,128]{0,2,3,1:T(2,128)(2,1)S(1)}, bf16[64,6,2,128]{0,2,3,1:T(2,128)(2,1)S(1)}, u32[]{:S(2)}, u32[]{:S(2)}) collective-permute-start(bf16[64,6,2,128]{0,2,3,1:T(2,128)(2,1)S(1)} %pad_maximum_fusion.5), channel_id=1, source_target_pairs={{0,2},{2,0},{1,3},{3,1},{4,6},{6,4},{5,7},{7,5},{8,10},{10,8},{9,1... | collective-permute-start | bytes 589832 | tf_op jit(solution)/shard_map/ppermute | solution.py:13
  146.7 17.4 %collective-permute-start.21 = (bf16[64,6,2,128]{0,2,3,1:T(2,128)(2,1)S(1)}, bf16[64,6,2,128]{0,2,3,1:T(2,128)(2,1)S(1)}, u32[]{:S(2)}, u32[]{:S(2)}) collective-permute-start(bf16[64,6,2,128]{0,2,3,1:T(2,128)(2,1)S(1)} %pad_maximum_fusion.5), channel_id=1, source_target_pairs={{2,0},{0,2},{3,1},{1,3},{6,4},{4,6},{7,5},{5,7},{10,8},{8,10},{11,... | collective-permute-start | bytes 589832 | tf_op jit(solution)/shard_map/ppermute | solution.py:16
  175.2 6.8 %collective-permute-start.24 = (bf16[64,2,2,128]{3,0,2,1:T(8,128)(2,1)S(1)}, bf16[64,2,2,128]{3,0,2,1:T(8,128)(2,1)S(1)}, u32[]{:S(2)}, u32[]{:S(2)}) collective-permute-start(bf16[64,2,2,128]{3,0,2,1:T(8,128)(2,1)S(1)} %get-tuple-element.14), channel_id=1, source_target_pairs={{0,4},{4,8},{8,12},{12,0},{1,5},{5,9},{9,13},{13,1},{2,6},{6,10},{... | collective-permute-start | bytes 196616 | tf_op jit(solution)/shard_map/ppermute | solution.py:13
  182.8 7.8 %collective-permute-start.26 = (bf16[64,6,2,128]{3,0,2,1:T(8,128)(2,1)S(1)}, bf16[64,6,2,128]{3,0,2,1:T(8,128)(2,1)S(1)}, u32[]{:S(2)}, u32[]{:S(2)}) collective-permute-start(bf16[64,6,2,128]{3,0,2,1:T(8,128)(2,1)S(1)} %pad_maximum_fusion.9), channel_id=1, source_target_pairs={{0,2},{2,0},{1,3},{3,1},{4,6},{6,4},{5,7},{7,5},{8,10},{10,8},{9,1... | collective-permute-start | bytes 589832 | tf_op jit(solution)/shard_map/ppermute | solution.py:13
  184.4 9.5 %collective-permute-start.27 = (bf16[64,6,2,128]{3,0,2,1:T(8,128)(2,1)S(1)}, bf16[64,6,2,128]{3,0,2,1:T(8,128)(2,1)S(1)}, u32[]{:S(2)}, u32[]{:S(2)}) collective-permute-start(bf16[64,6,2,128]{3,0,2,1:T(8,128)(2,1)S(1)} %pad_maximum_fusion.9), channel_id=1, source_target_pairs={{2,0},{0,2},{3,1},{1,3},{6,4},{4,6},{7,5},{5,7},{10,8},{8,10},{11,... | collective-permute-start | bytes 589832 | tf_op jit(solution)/shard_map/ppermute | solution.py:16
  204.3 8.3 %collective-permute-start.30 = (bf16[64,2,2,128]{0,2,3,1:T(2,128)(2,1)S(1)}, bf16[64,2,2,128]{0,2,3,1:T(2,128)(2,1)S(1)}, u32[]{:S(2)}, u32[]{:S(2)}) collective-permute-start(bf16[64,2,2,128]{0,2,3,1:T(2,128)(2,1)S(1)} %slice_bitcast_fusion.1), channel_id=1, source_target_pairs={{0,4},{4,8},{8,12},{12,0},{1,5},{5,9},{9,13},{13,1},{2,6},{6,10},{... | collective-permute-start | bytes 196616 | tf_op jit(solution)/shard_map/ppermute | solution.py:13
  204.6 8.5 %collective-permute-start.31 = (bf16[64,2,2,128]{0,2,3,1:T(2,128)(2,1)S(1)}, bf16[64,2,2,128]{0,2,3,1:T(2,128)(2,1)S(1)}, u32[]{:S(2)}, u32[]{:S(2)}) collective-permute-start(bf16[64,2,2,128]{0,2,3,1:T(2,128)(2,1)S(1)} %slice_bitcast_fusion.1), channel_id=1, source_target_pairs={{4,0},{8,4},{12,8},{0,12},{5,1},{9,5},{13,9},{1,13},{6,2},{10,6},{... | collective-permute-start | bytes 196616 | tf_op jit(solution)/shard_map/ppermute | solution.py:16
  213.8 12.1 %collective-permute-start.32 = (bf16[64,6,2,128]{0,2,3,1:T(2,128)(2,1)S(1)}, bf16[64,6,2,128]{0,2,3,1:T(2,128)(2,1)S(1)}, u32[]{:S(2)}, u32[]{:S(2)}) collective-permute-start(bf16[64,6,2,128]{0,2,3,1:T(2,128)(2,1)S(1)} %pad_maximum_fusion.6), channel_id=1, source_target_pairs={{0,2},{2,0},{1,3},{3,1},{4,6},{6,4},{5,7},{7,5},{8,10},{10,8},{9,1... | collective-permute-start | bytes 589832 | tf_op jit(solution)/shard_map/ppermute | solution.py:13
  215.4 17.0 %collective-permute-start.33 = (bf16[64,6,2,128]{0,2,3,1:T(2,128)(2,1)S(1)}, bf16[64,6,2,128]{0,2,3,1:T(2,128)(2,1)S(1)}, u32[]{:S(2)}, u32[]{:S(2)}) collective-permute-start(bf16[64,6,2,128]{0,2,3,1:T(2,128)(2,1)S(1)} %pad_maximum_fusion.6), channel_id=1, source_target_pairs={{2,0},{0,2},{3,1},{1,3},{6,4},{4,6},{7,5},{5,7},{10,8},{8,10},{11,... | collective-permute-start | bytes 589832 | tf_op jit(solution)/shard_map/ppermute | solution.py:16
  243.9 6.8 %collective-permute-start.36 = (bf16[64,2,2,128]{3,0,2,1:T(8,128)(2,1)S(1)}, bf16[64,2,2,128]{3,0,2,1:T(8,128)(2,1)S(1)}, u32[]{:S(2)}, u32[]{:S(2)}) collective-permute-start(bf16[64,2,2,128]{3,0,2,1:T(8,128)(2,1)S(1)} %get-tuple-element.12), channel_id=1, source_target_pairs={{0,4},{4,8},{8,12},{12,0},{1,5},{5,9},{9,13},{13,1},{2,6},{6,10},{... | collective-permute-start | bytes 196616 | tf_op jit(solution)/shard_map/ppermute | solution.py:13
  244.5 6.6 %collective-permute-start.37 = (bf16[64,2,2,128]{3,0,2,1:T(8,128)(2,1)S(1)}, bf16[64,2,2,128]{3,0,2,1:T(8,128)(2,1)S(1)}, u32[]{:S(2)}, u32[]{:S(2)}) collective-permute-start(bf16[64,2,2,128]{3,0,2,1:T(8,128)(2,1)S(1)} %get-tuple-element.12), channel_id=1, source_target_pairs={{4,0},{8,4},{12,8},{0,12},{5,1},{9,5},{13,9},{1,13},{6,2},{10,6},{... | collective-permute-start | bytes 196616 | tf_op jit(solution)/shard_map/ppermute | solution.py:16
  251.1 7.8 %collective-permute-start.38 = (bf16[64,6,2,128]{3,0,2,1:T(8,128)(2,1)S(1)}, bf16[64,6,2,128]{3,0,2,1:T(8,128)(2,1)S(1)}, u32[]{:S(2)}, u32[]{:S(2)}) collective-permute-start(bf16[64,6,2,128]{3,0,2,1:T(8,128)(2,1)S(1)} %pad_maximum_fusion.10), channel_id=1, source_target_pairs={{0,2},{2,0},{1,3},{3,1},{4,6},{6,4},{5,7},{7,5},{8,10},{10,8},{9,1... | collective-permute-start | bytes 589832 | tf_op jit(solution)/shard_map/ppermute | solution.py:13
  252.6 8.8 %collective-permute-start.39 = (bf16[64,6,2,128]{3,0,2,1:T(8,128)(2,1)S(1)}, bf16[64,6,2,128]{3,0,2,1:T(8,128)(2,1)S(1)}, u32[]{:S(2)}, u32[]{:S(2)}) collective-permute-start(bf16[64,6,2,128]{3,0,2,1:T(8,128)(2,1)S(1)} %pad_maximum_fusion.10), channel_id=1, source_target_pairs={{2,0},{0,2},{3,1},{1,3},{6,4},{4,6},{7,5},{5,7},{10,8},{8,10},{11,... | collective-permute-start | bytes 589832 | tf_op jit(solution)/shard_map/ppermute | solution.py:16
  271.8 8.3 %collective-permute-start.42 = (bf16[64,2,2,128]{0,2,3,1:T(2,128)(2,1)S(1)}, bf16[64,2,2,128]{0,2,3,1:T(2,128)(2,1)S(1)}, u32[]{:S(2)}, u32[]{:S(2)}) collective-permute-start(bf16[64,2,2,128]{0,2,3,1:T(2,128)(2,1)S(1)} %slice_bitcast_fusion), channel_id=1, source_target_pairs={{0,4},{4,8},{8,12},{12,0},{1,5},{5,9},{9,13},{13,1},{2,6},{6,10},{... | collective-permute-start | bytes 196616 | tf_op jit(solution)/shard_map/ppermute | solution.py:13
  273.2 8.6 %collective-permute-start.43 = (bf16[64,2,2,128]{0,2,3,1:T(2,128)(2,1)S(1)}, bf16[64,2,2,128]{0,2,3,1:T(2,128)(2,1)S(1)}, u32[]{:S(2)}, u32[]{:S(2)}) collective-permute-start(bf16[64,2,2,128]{0,2,3,1:T(2,128)(2,1)S(1)} %slice_bitcast_fusion), channel_id=1, source_target_pairs={{4,0},{8,4},{12,8},{0,12},{5,1},{9,5},{13,9},{1,13},{6,2},{10,6},{... | collective-permute-start | bytes 196616 | tf_op jit(solution)/shard_map/ppermute | solution.py:16
  282.4 12.1 %collective-permute-start.44 = (bf16[64,6,2,128]{0,2,3,1:T(2,128)(2,1)S(1)}, bf16[64,6,2,128]{0,2,3,1:T(2,128)(2,1)S(1)}, u32[]{:S(2)}, u32[]{:S(2)}) collective-permute-start(bf16[64,6,2,128]{0,2,3,1:T(2,128)(2,1)S(1)} %pad_maximum_fusion.7), channel_id=1, source_target_pairs={{0,2},{2,0},{1,3},{3,1},{4,6},{6,4},{5,7},{7,5},{8,10},{10,8},{9,1... | collective-permute-start | bytes 589832 | tf_op jit(solution)/shard_map/ppermute | solution.py:13
  284.0 17.5 %collective-permute-start.45 = (bf16[64,6,2,128]{0,2,3,1:T(2,128)(2,1)S(1)}, bf16[64,6,2,128]{0,2,3,1:T(2,128)(2,1)S(1)}, u32[]{:S(2)}, u32[]{:S(2)}) collective-permute-start(bf16[64,6,2,128]{0,2,3,1:T(2,128)(2,1)S(1)} %pad_maximum_fusion.7), channel_id=1, source_target_pairs={{2,0},{0,2},{3,1},{1,3},{6,4},{4,6},{7,5},{5,7},{10,8},{8,10},{11,... | collective-permute-start | bytes 589832 | tf_op jit(solution)/shard_map/ppermute | solution.py:16
  (39 other events, 238.7 us)
where the time goes:
time: 320 us; the launch traced here: 314 us
  waiting for transfers between devices  131 us (41%)
  starting transfers between devices  55.5 us (17%)
  blocking collectives  44.6 us (14%)
  matrix products  33 us (10%)
  local copies, waits for them, and re-layouts  27.2 us (8%)
  other arithmetic  19.7 us (6%)
    ppermute x24, waiting for transfers between devices, padded_2(): lax.ppermute(lax.slice_in_dim(block, block.shape[dim] - width, None, axis...  88 us
    ppermute x24, waiting for transfers between devices, padded_2(): lax.ppermute(lax.slice_in_dim(block, 0, width, axis=dim), axis, backward)  43.5 us
    conv_general_dilated x16, matrix products, convolve(): lax.conv_general_dilated(padded[None], filters, (1, 1, 1), 'VALID', dimen...  33 us
    ppermute x24, starting transfers between devices, padded_2(): lax.ppermute(lax.slice_in_dim(block, 0, width, axis=dim), axis, backward)  32.4 us
    ppermute x24, starting transfers between devices, padded_2(): lax.ppermute(lax.slice_in_dim(block, block.shape[dim] - width, None, axis...  23.2 us
    all_gather x1, blocking collectives, on_device(): lax.all_gather(filter_in, 'gx', axis=0, tiled=True)  15.5 us
    all_gather x1, blocking collectives, on_device(): lax.all_gather(filter_out, 'gx', axis=0, tiled=True)  14.5 us
    broadcast_in_dim x8, other arithmetic, convolve(): padded[None]  14.3 us
  transfers between devices with their start and end apart: 48, of which 41 were waited for; matrix products, arithmetic and copies ran while one was open for 1% of the time, Pallas kernels for 0%

commit v1 on v0

v1 whole, which is shorter than its diff:
```python
import functools

import jax
import jax.numpy as jnp
from jax import lax
from jax.experimental import pallas as pl
from jax.experimental.pallas import tpu as pltpu
from jax.sharding import PartitionSpec as P

EDGE = 16
MESH = pl.DeviceIdType.MESH


def kernel(steps, sizes, pos_ref, mom_ref, noise_ref, w_ref, bias_ref,
           q_out, p_out, a1, a2, b1, b2, eq, eh, t_ref, q_ref, p_ref, send, recv, *gather):
    nx, ny, nz = sizes
    c = pos_ref.shape[0]
    inside = len(gather) > 0
    if inside:
        wg, wf, wsend, wrecv = gather
    x, z, lanes = q_ref.shape
    y = lanes // c
    full = eq.shape[1]
    wrap = ny == 2
    slots = eq.shape[2] // c
    own = slice(EDGE, EDGE + z)
    mine = slice(lanes, 2 * lanes)

    ix, iy, iz = lax.axis_index("gx"), lax.axis_index("gy"), lax.axis_index("gz")
    up = {"gx": lax.rem(ix + 1, nx), "gy": lax.rem(iy + 1, ny), "gz": lax.rem(iz + 1, nz)}
    down = {
        "gx": lax.rem(ix + nx - 1, nx),
        "gy": lax.rem(iy + ny - 1, ny),
        "gz": lax.rem(iz + nz - 1, nz),
    }

    def at_side(**which):
        return {axis: which[axis][axis] for axis in which}

    def early(buf):
        core = slice(2, 2 + x)
        low, high = slice(0, EDGE), slice(z + EDGE, full)
        block = buf.at[core, own, mine]
        edges = (
            (up, buf.at[core, z : z + EDGE, mine], low),
            (down, buf.at[core, EDGE : 2 * EDGE, mine], high),
        )
        out = []
        for side, source, rows in edges:
            out.append((at_side(gz=side), source, buf.at[core, rows, mine], True))
        for beside, part in others:
            out.append((at_side(gy=beside), block, buf.at[core, own, part], True))
            for side, source, rows in edges:
                target = buf.at[core, rows, part]
                out.append((at_side(gy=beside, gz=side), source, target, True))
        out.append((at_side(gx=up), buf.at[x : 2 + x, own, mine], buf.at[0:2, own, mine], False))
        out.append(
            (at_side(gx=down), buf.at[2:4, own, mine], buf.at[2 + x : 4 + x, own, mine], False)
        )
        return out

    def late(buf):
        low, high = slice(0, EDGE), slice(z + EDGE, full)
        areas = [(slice(0, full), part) for _, part in others] + [(low, mine), (high, mine)]
        out = []
        for rows, part in areas:
            for side, source, target in (
                (up, slice(x, 2 + x), slice(0, 2)),
                (down, slice(2, 4), slice(2 + x, 4 + x)),
            ):
                out.append(
                    (at_side(gx=side), buf.at[source, rows, part], buf.at[target, rows, part])
                )
        return out

    others = [(up, slice(0, lanes))]
    if not wrap:
        others.append((down, slice(2 * lanes, 3 * lanes)))

    def remote(source, target, sems, number, device):
        return pltpu.make_async_remote_copy(
            src_ref=source,
            dst_ref=target,
            send_sem=sems[0].at[number],
            recv_sem=sems[1].at[number],
            device_id=device,
            device_id_type=MESH,
        )

    peers = []
    if inside:
        for dx in range(nx):
            for dy in range(ny):
                if dx or dy:
                    peers.append({"gx": lax.rem(ix + dx, nx), "gy": lax.rem(iy + dy, ny)})
    barrier = pltpu.get_barrier_semaphore()
    greeted = peers + [device for device, _, _, _ in early(eq)]
    for device in greeted:
        pl.semaphore_signal(barrier, inc=1, device_id=device, device_id_type=MESH)
    pl.semaphore_wait(barrier, len(greeted))

    if inside:
        copies = []
        for number, device in enumerate(peers):
            copy = remote(w_ref, wg.at[iy, ix], (wsend, wrecv), number, device)
            copy.start()
            copies.append(copy)
        wg[iy, ix] = w_ref[...]
        for copy in copies:
            copy.wait()
        ci = c // ny
        for which in range(2):
            for at in range(27):
                columns = []
                for j in range(ny):
                    pieces = [wg[j, i, which, :, at * ci : (at + 1) * ci] for i in range(nx)]
                    columns.append(jnp.concatenate(pieces, axis=0))
                wf[which, at // 3, at % 3] = jnp.concatenate(columns, axis=1)
        filters = wf
    else:
        filters = w_ref

    def exchange(buf, bank):
        sems = (send.at[bank], recv.at[bank])
        first, own_x = [], []
        number = 0
        for device, source, target, passed in early(buf):
            copy = remote(source, target, sems, number, device)
            number += 1
            copy.start()
            (first if passed else own_x).append(copy)
        for copy in first:
            copy.wait_recv()
        second = []
        for device, source, target in late(buf):
            copy = remote(source, target, sems, number, device)
            number += 1
            copy.start()
            second.append(copy)
        for copy in own_x + second:
            copy.wait_recv()
        for copy in first + own_x + second:
            copy.wait_send()

    def slot(at):
        return at % slots

    def unfold(tap, carry):
        blank = jnp.zeros((c, c), jnp.bfloat16)

        def rows(out, which, at, flip, cols, pick):
            line = [blank] * cols
            for col, b in pick:
                line[col] = filters[which, at, 2 - b if flip else b]
            return jnp.concatenate(line, axis=1)

        back = 8 - tap
        for yo in range(y + 2):
            a1[tap, yo * c : (yo + 1) * c, :] = rows(
                a1, 0, tap, False, slots, [(slot(yo + b), b) for b in range(3)]
            )
        for yo in range(y):
            a2[tap, yo * c : (yo + 1) * c, :] = rows(
                a2, 1, tap, False, y + 2, [(yo + b, b) for b in range(3)]
            )
        for s in range(slots):
            pick = [(yo, b) for yo in range(y + 2) for b in range(3) if slot(yo + b) == s]
            b2[tap, s * c : (s + 1) * c, :] = rows(b2, 1, back, True, y + 2, pick)
        for yi in range(y + 2):
            pick = [(yo, yi - yo) for yo in range(y) if 0 <= yi - yo <= 2]
            b1[tap, yi * c : (yi + 1) * c, :] = rows(b1, 0, back, True, y, pick)
        return carry

    lax.fori_loop(0, 9, unfold, 0)

    def load(ref2d, at):
        span = [ref2d[:, (at * y + j) * z : (at * y + j + 1) * z] for j in range(y)]
        return jnp.concatenate(span, axis=0).astype(jnp.float32).T

    for at in range(x):
        q_ref[at] = load(pos_ref, at)
        p_ref[at] = load(mom_ref, at)

    def conv(source, weights, out_x, transposed):
        width = source.shape[2]
        total = None
        for tz in range(3):
            part = None
            for tx in range(3):
                left = source[tx : tx + out_x].reshape(out_x * full, width)
                term = lax.dot_general(
                    left,
                    weights[tx * 3 + tz],
                    (((1,), (1 if transposed else 0,)), ((), ())),
                    preferred_element_type=jnp.float32,
                )
                part = term if part is None else part + term
            if tz != 1:
                part = pltpu.roll(part, 1 if tz == 0 else out_x * full - 1, 0)
            total = part if total is None else total + part
        return total.reshape(out_x, full, total.shape[-1])

    step = 0.25
    decay = jnp.exp(jnp.float32(-0.25))
    kick = jnp.sqrt(1.0 - decay * decay)

    def body(k, carry):
        eq[2 : 2 + x, own, mine] = q_ref[...].astype(jnp.bfloat16)
        exchange(eq, 0)
        t_ref[...] = jnp.tanh(conv(eq, a1, x + 2, True) + bias_ref[...][None])
        h2 = conv(t_ref[...].astype(jnp.bfloat16), a2, x, True)
        eh[2 : 2 + x, own, mine] = h2[:, own].astype(jnp.bfloat16)
        exchange(eh, 1)
        gu = conv(eh, b2, x + 2, False)
        t = t_ref[...]
        gh = (gu * (1.0 - t * t)).astype(jnp.bfloat16)
        force = conv(gh, b1, x, False)[:, own] + q_ref[...]
        half = 0.5 * step

        @pl.when(k > 0)
        def _():
            p_ref[...] = p_ref[...] - half * force

        @pl.when(k < steps)
        def _():
            p = p_ref[...] - half * force
            q = q_ref[...] + half * p
            now = noise_ref.at[k]
            drawn = jnp.stack([load(now, at) for at in range(x)])
            p = decay * p + kick * drawn
            q_ref[...] = q + half * p
            p_ref[...] = p

        return carry

    lax.fori_loop(0, steps + 1, body, 0)

    for ref, out in ((q_ref, q_out), (p_ref, p_out)):
        for at in range(x):
            flat = ref[at].T
            for j in range(y):
                out[:, (at * y + j) * z : (at * y + j + 1) * z] = flat[j * c : (j + 1) * c]


def on_device(sizes, position, momentum, noise, filter_in, filter_out, bias):
    nx, ny, nz = sizes
    c, x, y, z = position.shape
    steps = noise.shape[0]
    assert x >= 2 and y == 2 and z % EDGE == 0 and nx > 2 and ny > 1
    both = jnp.stack([filter_in, filter_out])
    co, ci = both.shape[1], both.shape[2]
    gather = []
    if co % EDGE == 0:
        both = both.transpose(0, 1, 3, 5, 4, 2).reshape(2, co, 27 * ci)
        gather = [
            pltpu.VMEM((ny, nx, 2, co, 27 * ci), jnp.bfloat16),
            pltpu.VMEM((2, 9, 3, c, c), jnp.bfloat16),
            pltpu.SemaphoreType.DMA((nx * ny - 1,)),
            pltpu.SemaphoreType.DMA((nx * ny - 1,)),
        ]
    else:
        both = both.reshape(2 * co, ci * 27)
        both = lax.all_gather(both, ("gx", "gy"), axis=0, tiled=True)
        both = both.reshape(nx, ny, 2, co, ci, 3, 3, 3)
        both = both.transpose(2, 5, 7, 6, 0, 3, 1, 4).reshape(2, 9, 3, c, c)
    lanes = y * c
    slots = 2 * y if ny == 2 else 3 * y
    full = z + 2 * EDGE
    wide = (y + 2) * c
    flat = jax.ShapeDtypeStruct((c, x * y * z), jnp.float32)
    copies = 13 if ny == 2 else 18
    vmem = pl.BlockSpec(memory_space=pltpu.VMEM)
    q, p = pl.pallas_call(
        functools.partial(kernel, steps, sizes),
        out_shape=(flat, flat),
        in_specs=[vmem] * 5,
        out_specs=(vmem, vmem),
        scratch_shapes=[
            pltpu.VMEM((9, wide, slots * c), jnp.bfloat16),
            pltpu.VMEM((9, lanes, wide), jnp.bfloat16),
            pltpu.VMEM((9, wide, lanes), jnp.bfloat16),
            pltpu.VMEM((9, slots * c, wide), jnp.bfloat16),
            pltpu.VMEM((x + 4, full, slots * c), jnp.bfloat16),
            pltpu.VMEM((x + 4, full, slots * c), jnp.bfloat16),
            pltpu.VMEM((x + 2, full, wide), jnp.float32),
            pltpu.VMEM((x, z, lanes), jnp.float32),
            pltpu.VMEM((x, z, lanes), jnp.float32),
            pltpu.SemaphoreType.DMA((2, copies)),
            pltpu.SemaphoreType.DMA((2, copies)),
            *gather,
        ],
        compiler_params=pltpu.CompilerParams(
            collective_id=0, has_side_effects=True, vmem_limit_bytes=56 * 2**20
        ),
    )(
        position.reshape(c, -1),
        momentum.reshape(c, -1),
        noise.reshape(steps, c, -1),
        both,
        jnp.tile(bias, y + 2)[None],
    )
    return q.reshape(position.shape), p.reshape(momentum.shape)


def solution(mesh):
    field = P(None, ("grp", "gx"), "gy", "gz")
    filters = P("gx", "gy", None, None, None)
    sizes = tuple(mesh.shape[name] for name in ("gx", "gy", "gz"))
    return jax.shard_map(
        functools.partial(on_device, sizes),
        mesh=mesh,
        in_specs=(field, field, P(None, None, ("grp", "gx"), "gy", "gz"), filters, filters, P()),
        out_specs=(field, field),
        check_vma=False,
    )
```

time: 320 us -> 126 us (0.39); the launches traced: 314 us -> 126 us
  waiting for transfers between devices: 131 us -> 0 us
  Pallas kernels: 0 us -> 117 us
  starting transfers between devices: 55.5 us -> 0 us
  blocking collectives: 44.6 us -> 0 us
  matrix products: 33 us -> 0 us
  local copies, waits for them, and re-layouts: 27.2 us -> 6.69 us
  other arithmetic: 19.7 us -> 1 us
    ppermute x48 -> x0, waiting for transfers between devices: 131 us -> none  [the longest x24 88 us: padded_2(): lax.ppermute(lax.slice_in_dim(block, block.shape[dim] - width, None, axis...]
    pallas_call x0 -> x1, Pallas kernels: none -> 117 us  [on_device(): pl.pallas_call(functools.partial(kernel, steps, sizes), out_shape=(flat,...]
    ppermute x48 -> x0, starting transfers between devices: 55.5 us -> none  [the longest x24 32.4 us: padded_2(): lax.ppermute(lax.slice_in_dim(block, 0, width, axis=dim), axis, backward)]
    all_gather x4 -> x0, blocking collectives: 44.6 us -> none  [the longest x1 15.5 us: on_device(): lax.all_gather(filter_in, 'gx', axis=0, tiled=True)]
    conv_general_dilated x16 -> x0, matrix products: 33 us -> none  [convolve(): lax.conv_general_dilated(padded[None], filters, (1, 1, 1), 'VALID', dimen...]
    broadcast_in_dim x8 -> x0, other arithmetic: 14.3 us -> none  [convolve(): padded[None]]
    unnamed x56 -> x10, local copies, waits for them, and re-layouts: 13.5 us -> 0.41 us
    reshape x0 -> x6, local copies, waits for them, and re-layouts: none -> 5.49 us  [the longest x2 2.41 us: on_device(): return (q.reshape(position.shape), p.reshape(momentum.shape))]
  transfers between devices with their start and end apart: 48 -> 0, of which waited for: 41 -> 0; matrix products, arithmetic and copies ran while one was open for 1% -> 0% of each run, Pallas kernels for 0% -> 0%
where the time goes in v1:
time: 126 us
  Pallas kernels  117 us (93%)
  local copies, waits for them, and re-layouts  6.69 us (5%)
    pallas_call x1, Pallas kernels, on_device(): pl.pallas_call(functools.partial(kernel, steps, sizes), out_shape=(flat,...  117 us

profile of v1, /device:TPU:0, one launch (start us, length us, event | category | flops | bytes accessed | tf_op | source)
XLA Modules:
  0.0 125.5 jit_solution(4449645082163691080)
XLA Ops:
  0.6 1.0 maximum_bitcast_fusion
  1.6 0.1 copy.9
  1.8 0.0 copy-start
  1.8 0.8 reshape.26.w_ref
  2.6 0.1 copy-done
  2.7 0.0 copy-start.1
  2.7 0.7 reshape.25.noise_ref
  3.4 0.2 copy-done.1
  3.6 0.0 copy-start.2
  3.6 0.8 reshape.23.pos_ref
  4.4 0.1 copy-done.2
  4.5 0.0 copy-start.4
  4.5 0.8 reshape.24.mom_ref
  5.3 0.0 copy-done.4
  5.3 0.7 broadcast_in_dim_tile.3.bias_ref
  5.9 117.2 %shard_map.77 = (f32[64,512]{1,0:T(8,128)}, f32[64,512]{1,0:T(8,128)}) custom-call(f32[64,512]{1,0:T(8,128)} %reshape.23.pos_ref, f32[64,512]{1,0:T(8,128)} %reshape.24.mom_ref, bf16[3,64,512]{2,1,0:T(8,128)(2,1)} %reshape.25.noise_ref, bf16[2,16,864]{2,1,0:T(8,128)(2,1)} %reshape.26.w_ref, f32[1,256]{1,0:T(1,128)} %broadcast_in_dim_tile.3.bias_ref), custom_call_target="tpu_custom_call" | custom-call | tf_op jit(solution)/shard_map/pallas_call | solution.py:273
  123.1 0.0 copy-start.3
  123.1 1.7 %reshape.27 = f32[64,2,2,128]{3,2,1,0:T(2,128)} reshape(f32[64,512]{1,0:T(8,128)} %get-tuple-element.4) | data formatting | bytes 262144 | tf_op jit(solution)/shard_map/reshape | solution.py:302
  124.8 0.0 copy-done.3
  124.8 0.7 reshape.28
  (1 shorter events, 0.0 us)
Async XLA Ops:
  1.8 0.9 copy-start
  2.7 0.9 copy-start.1
  3.6 0.9 copy-start.2
  4.5 0.8 copy-start.4
  123.1 1.7 %copy-start.3 = (f32[64,512]{1,0:T(8,128)S(1)}, f32[64,512]{1,0:T(8,128)}, u32[]{:S(2)}) copy-start(f32[64,512]{1,0:T(8,128)} %get-tuple-element.5) | copy-start | bytes 393220

commit v2 on v1

--- a/solution.py
+++ b/solution.py
@@ -53,25 +53,33 @@
             for side, source, rows in edges:
                 target = buf.at[core, rows, part]
                 out.append((at_side(gy=beside, gz=side), source, target, True))
-        out.append((at_side(gx=up), buf.at[x : 2 + x, own, mine], buf.at[0:2, own, mine], False))
         out.append(
             (at_side(gx=down), buf.at[2:4, own, mine], buf.at[2 + x : 4 + x, own, mine], False)
         )
+        out.append((at_side(gx=up), buf.at[x : 2 + x, own, mine], buf.at[0:2, own, mine], False))
         return out
 
     def late(buf):
         low, high = slice(0, EDGE), slice(z + EDGE, full)
-        areas = [(slice(0, full), part) for _, part in others] + [(low, mine), (high, mine)]
-        out = []
-        for rows, part in areas:
-            for side, source, target in (
-                (up, slice(x, 2 + x), slice(0, 2)),
-                (down, slice(2, 4), slice(2 + x, 4 + x)),
-            ):
-                out.append(
-                    (at_side(gx=side), buf.at[source, rows, part], buf.at[target, rows, part])
-                )
-        return out
+        from_low = (up, slice(x, 2 + x), slice(0, 2))
+        from_high = (down, slice(2, 4), slice(2 + x, 4 + x))
+        plan = []
+        for _, part in others:
+            plan.append((from_low, slice(0, full), part))
+            plan += [(from_high, low, part), (from_high, high, part)]
+        for side in (from_low, from_high):
+            plan += [(side, low, mine), (side, high, mine)]
+        return [
+            (at_side(gx=side), buf.at[source, rows, part], buf.at[target, rows, part])
+            for (side, source, target), rows, part in plan
+        ]
+
+    def forward(buf):
+        planes = slice(2 + x, 4 + x)
+        return [
+            (at_side(gy=beside), buf.at[planes, own, mine], buf.at[planes, own, part])
+            for beside, part in others
+        ]
 
     others = [(up, slice(0, lanes))]
     if not wrap:
@@ -137,7 +145,13 @@
             number += 1
             copy.start()
             second.append(copy)
-        for copy in own_x + second:
+        own_x[0].wait_recv()
+        for device, source, target in forward(buf):
+            copy = remote(source, target, sems, number, device)
+            number += 1
+            copy.start()
+            second.append(copy)
+        for copy in own_x[1:] + second:
             copy.wait_recv()
         for copy in first + own_x + second:
             copy.wait_send()
@@ -268,7 +282,7 @@
     full = z + 2 * EDGE
     wide = (y + 2) * c
     flat = jax.ShapeDtypeStruct((c, x * y * z), jnp.float32)
-    copies = 13 if ny == 2 else 18
+    copies = 15 if ny == 2 else 24
     vmem = pl.BlockSpec(memory_space=pltpu.VMEM)
     q, p = pl.pallas_call(
         functools.partial(kernel, steps, sizes),

time: 126 us -> 115 us (0.913)
  Pallas kernels: 117 us -> 106 us
    pallas_call x1, Pallas kernels: 117 us -> 106 us  [on_device(): pl.pallas_call(functools.partial(kernel, steps, sizes), out_shape=(flat,...]
where the time goes in v2:
time: 115 us; the launch traced here: 114 us
  Pallas kernels  106 us (92%)
  local copies, waits for them, and re-layouts  6.69 us (6%)
    pallas_call x1, Pallas kernels, on_device(): pl.pallas_call(functools.partial(kernel, steps, sizes), out_shape=(flat,...  106 us
    reshape x2, local copies, waits for them, and re-layouts, on_device(): return (q.reshape(position.shape), p.reshape(momentum.shape))  2.41 us

profile of v2, /device:TPU:0, one launch (start us, length us, event | category | flops | bytes accessed | tf_op | source)
XLA Modules:
  0.0 114.5 jit_solution(562578487603913163)
XLA Ops:
  0.6 1.0 maximum_bitcast_fusion
  1.6 0.1 copy.9
  1.8 0.0 copy-start
  1.8 0.8 reshape.26.w_ref
  2.6 0.1 copy-done
  2.7 0.0 copy-start.1
  2.7 0.7 reshape.25.noise_ref
  3.4 0.2 copy-done.1
  3.6 0.0 copy-start.2
  3.6 0.8 reshape.23.pos_ref
  4.4 0.1 copy-done.2
  4.5 0.0 copy-start.4
  4.5 0.8 reshape.24.mom_ref
  5.3 0.0 copy-done.4
  5.3 0.7 broadcast_in_dim_tile.3.bias_ref
  5.9 106.1 %shard_map.77 = (f32[64,512]{1,0:T(8,128)}, f32[64,512]{1,0:T(8,128)}) custom-call(f32[64,512]{1,0:T(8,128)} %reshape.23.pos_ref, f32[64,512]{1,0:T(8,128)} %reshape.24.mom_ref, bf16[3,64,512]{2,1,0:T(8,128)(2,1)} %reshape.25.noise_ref, bf16[2,16,864]{2,1,0:T(8,128)(2,1)} %reshape.26.w_ref, f32[1,256]{1,0:T(1,128)} %broadcast_in_dim_tile.3.bias_ref), custom_call_target="tpu_custom_call" | custom-call | tf_op jit(solution)/shard_map/pallas_call | solution.py:287
  112.1 0.0 copy-start.3
  112.1 1.7 %reshape.27 = f32[64,2,2,128]{3,2,1,0:T(2,128)} reshape(f32[64,512]{1,0:T(8,128)} %get-tuple-element.4) | data formatting | bytes 262144 | tf_op jit(solution)/shard_map/reshape | solution.py:316
  113.8 0.0 copy-done.3
  113.8 0.7 reshape.28
  (1 shorter events, 0.0 us)
Async XLA Ops:
  1.8 0.9 copy-start
  2.7 0.9 copy-start.1
  3.6 0.9 copy-start.2
  4.5 0.8 copy-start.4
  112.1 1.7 %copy-start.3 = (f32[64,512]{1,0:T(8,128)S(1)}, f32[64,512]{1,0:T(8,128)}, u32[]{:S(2)}) copy-start(f32[64,512]{1,0:T(8,128)} %get-tuple-element.5) | copy-start | bytes 393220
